TPU v7x, 32 devices: a whole 2x2x4 slice. The times are simulated.
32 devices in a mesh: mem: 16 (over z, y, x), rep: 2 (over core).
Axes of the slice: x: 2, y: 2, z: 4, core: 2. Of those that a mesh axis runs over, the one named last changes fastest.
Arguments:
- particle_vectors: bfloat16 [64, 131072], P('mem', 'rep'), may hold values from -6 to 6
- observed: bfloat16 [64, 131072], P('mem', 'rep'), may hold values from -24 to 24
- precision: float32 [131072], P('rep'), may hold values from 0.5 to 240, as said below
- entry_projection_matrix: bfloat16 [2, 256, 1024], replicated, may hold values from -0.375 to 0.375
- entry_offsets: float32 [2, 1024], replicated, may hold values from -3 to 3
- exit_projection_matrix: bfloat16 [2, 1024, 256], replicated, may hold values from -0.1875 to 0.1875
- exit_offsets: float32 [2, 256], replicated, may hold values from -3 to 3
Outputs:
- updated: bfloat16 [64, 131072], P('mem', 'rep')
Inputs may be any that keep to these rules, and one draw needn't show every extreme that they name: `precision`: positive precisions.
All inputs are finite; a program needn't handle non-finite values.
Results may differ from a plain program's by a relative error of at most 0.0065.
Values may be sent and summed in bfloat16 or wider, within the bound.
No kernel may reach another device: no remote copies, remote signals or barrier semaphores. Data moves between devices by JAX's collectives and lax.ppermute only.
A program may use at most 64 MiB of HBM per device.

v0:
```python
import jax
import jax.numpy as jnp
from jax import lax
from jax.sharding import PartitionSpec as P

PW = 256
LAYERS = 2


def contract(left, right):
    return lax.dot_general(
        left, right, (((1,), (1,)), ((), ())), preferred_element_type=jnp.float32
    )


def body(
    particle_vectors,
    observed,
    precision,
    entry_projection_matrix,
    entry_offsets,
    exit_projection_matrix,
    exit_offsets,
):
    owned, local_width = particle_vectors.shape
    stream = particle_vectors.reshape(owned * local_width // PW, PW)
    for layer in range(LAYERS):
        pre = (
            jnp.dot(stream, entry_projection_matrix[layer], preferred_element_type=jnp.float32)
            + entry_offsets[layer]
        )
        hidden = jax.nn.silu(pre).astype(jnp.bfloat16)
        stream = (
            stream.astype(jnp.float32)
            + jnp.dot(hidden, exit_projection_matrix[layer], preferred_element_type=jnp.float32)
            + exit_offsets[layer]
        ).astype(jnp.bfloat16)
    particle_outcomes = stream.reshape(owned, local_width)
    resid = (observed.astype(jnp.float32) - particle_outcomes.astype(jnp.float32)).astype(
        jnp.bfloat16
    )
    resid_wide = resid.astype(jnp.float32)
    mem_count = lax.axis_size("mem")
    member_total = owned * mem_count
    state_total = local_width * lax.axis_size("rep")
    misfit_local = jnp.sum(resid_wide * resid_wide * precision)
    damping = lax.psum(misfit_local, ("mem", "rep")) / (member_total * state_total) + 1e-06
    own_states, own_preds, own_resid = (
        lax.all_to_all(particle_vectors, "mem", split_axis=1, concat_axis=0, tiled=True),
        lax.all_to_all(particle_outcomes, "mem", split_axis=1, concat_axis=0, tiled=True),
        lax.all_to_all(resid, "mem", split_axis=1, concat_axis=0, tiled=True),
    )
    block_width = own_states.shape[1]
    prec_block = lax.dynamic_slice_in_dim(
        precision, lax.axis_index("mem") * block_width, block_width
    )
    pred_wide = own_preds.astype(jnp.float32)
    pred_dev = (pred_wide - jnp.mean(pred_wide, axis=0)).astype(jnp.bfloat16)
    state_wide = own_states.astype(jnp.float32)
    state_dev = (state_wide - jnp.mean(state_wide, axis=0)).astype(jnp.bfloat16)
    weighted = (pred_dev.astype(jnp.float32) * prec_block).astype(jnp.bfloat16)
    gram = lax.psum(contract(weighted, pred_dev), ("mem", "rep")) / state_total
    cross = (
        lax.psum_scatter(
            contract(own_resid, weighted), ("mem", "rep"), scatter_dimension=0, tiled=True
        )
        / state_total
    )
    kmat = gram + damping * jnp.eye(member_total, dtype=jnp.float32)
    factor = jnp.linalg.cholesky(kmat)
    middle = jax.scipy.linalg.solve_triangular(factor, cross.T, lower=True)
    solved = jax.scipy.linalg.solve_triangular(factor, middle, lower=True, trans="T")
    mixing = solved.T.astype(jnp.bfloat16)
    fresh = (
        state_wide
        + jnp.dot(
            lax.all_gather(mixing, ("mem", "rep"), axis=0, tiled=True),
            state_dev,
            preferred_element_type=jnp.float32,
        )
    ).astype(jnp.bfloat16)
    return lax.all_to_all(fresh, "mem", split_axis=0, concat_axis=1, tiled=True)


def solution(mesh):
    placed = (P("mem", "rep"), P("mem", "rep"), P("rep"), P(), P(), P(), P())
    return jax.shard_map(
        body, mesh=mesh, in_specs=placed, out_specs=P("mem", "rep"), check_vma=False
    )
```

profile of v0, /device:TPU:0, one launch (start us, length us, event | category | flops | bytes accessed | tf_op | source)
XLA Modules:
  0.0 171.0 jit_solution(16117873625604666661)
XLA Ops:
  0.0 0.0 copy-start.2
  0.0 0.8 fusion.32
  0.8 0.8 fusion.33
  1.6 1.4 reshape.69
  3.0 0.0 copy-done.2
  3.0 2.5 %fusion.3 = bf16[1024,256]{1,0:T(8,128)(2,1)S(1)} fusion(bf16[1024,256]{1,0:T(8,128)(2,1)S(1)} %reshape.69, f32[1024]{0:T(1024)S(1)} %bitcast.55, f32[256]{0:T(256)S(1)} %bitcast.57, bf16[2,1024,256]{2,1,0:T(8,128)(2,1)S(1)} %copy-done.2, bf16[2,256,1024]{2,1,0:T(8,128)(2,1)} %param.10), kind=kOutput, calls=%fused_computation.12 | convolution fusion | flops 1081081856 | bytes 2626560 | tf_op jit(solution)/shard_map/dot_general | solution.py:35
  5.5 2.5 %fusion.4 = bf16[1024,256]{1,0:T(8,128)(2,1)S(1)} fusion(bf16[1024,256]{1,0:T(8,128)(2,1)S(1)} %fusion.3, f32[1024]{0:T(1024)S(1)} %bitcast.54, f32[256]{0:T(256)S(1)} %bitcast.56, bf16[2,1024,256]{2,1,0:T(8,128)(2,1)S(1)} %copy-done.2, bf16[2,256,1024]{2,1,0:T(8,128)(2,1)} %param.10), kind=kOutput, calls=%fused_computation.13 | convolution fusion | flops 1081081856 | bytes 2626560 | tf_op jit(solution)/shard_map/dot_general | solution.py:35
  8.0 0.2 all_to_all.50
  8.2 1.2 copy.17
  9.4 8.3 %all-to-all-start.1 = ((bf16[4,16,4096]{2,0,1:T(4,128)(2,1)}), bf16[4,16,4096]{2,0,1:T(4,128)(2,1)S(1)}, u32[]{:S(2)}, u32[]{:S(2)}) async-start(bf16[4,16,4096]{2,0,1:T(4,128)(2,1)} %copy.17), calls=%async_computation.1 | async-start | bytes 1048576 | tf_op jit(solution)/shard_map/all_to_all | solution.py:50
  17.8 0.0 copy-start
  17.8 0.0 copy-start.1
  17.8 0.5 reshape.71
  18.3 0.5 copy-done
  18.8 0.1 copy-done.1
  18.9 1.9 %multiply_reduce_fusion = (f32[]{:T(128)}, bf16[4,65536]{1,0:T(4,128)(2,1)}) fusion(f32[65536]{0:T(1024)S(1)} %copy-done.1, f32[4,65536]{1,0:T(4,128)S(1)} %reshape.71, bf16[4,65536]{1,0:T(4,128)(2,1)S(1)} %copy-done), kind=kLoop, calls=%fused_computation.18 | loop fusion | flops 1835007 | bytes 2359300 | tf_op jit(solution)/shard_map/reduce_sum | solution.py:46
  20.7 0.0 dynamic-slice-start
  20.7 12.1 %all-to-all-done.1 = bf16[4,16,4096]{2,0,1:T(4,128)(2,1)S(1)} async-done(((bf16[4,16,4096]{2,0,1:T(4,128)(2,1)}), bf16[4,16,4096]{2,0,1:T(4,128)(2,1)S(1)}, u32[]{:S(2)}, u32[]{:S(2)}) %all-to-all-start.1) | async-done | bytes 524320 | tf_op jit(solution)/shard_map/all_to_all | solution.py:50
  32.8 3.9 %all-to-all-start.2 = ((bf16[4,16,4096]{2,0,1:T(4,128)(2,1)}), bf16[4,16,4096]{2,0,1:T(4,128)(2,1)S(1)}, u32[]{:S(2)}, u32[]{:S(2)}) async-start(bf16[4,16,4096]{2,0,1:T(4,128)(2,1)} %bitcast.14), calls=%async_computation.2 | async-start | bytes 1048576 | tf_op jit(solution)/shard_map/all_to_all | solution.py:51
  36.8 0.2 convert_reduce_fusion.1
  37.1 0.0 dynamic-slice-done
  37.1 0.5 multiply_convert_fusion.2
  37.6 0.1 convert_element_type.101
  37.7 0.1 convert_element_type.102
  37.9 13.4 %all-to-all-done.2 = bf16[4,16,4096]{2,0,1:T(4,128)(2,1)S(1)} async-done(((bf16[4,16,4096]{2,0,1:T(4,128)(2,1)}), bf16[4,16,4096]{2,0,1:T(4,128)(2,1)S(1)}, u32[]{:S(2)}, u32[]{:S(2)}) %all-to-all-start.2) | async-done | bytes 524320 | tf_op jit(solution)/shard_map/all_to_all | solution.py:51
  51.2 3.9 %all-to-all-start = ((bf16[4,16,4096]{2,0,1:T(4,128)(2,1)}), bf16[4,16,4096]{2,0,1:T(4,128)(2,1)S(1)}, u32[]{:S(2)}, u32[]{:S(2)}) async-start(bf16[4,16,4096]{2,0,1:T(4,128)(2,1)} %bitcast), calls=%async_computation | async-start | bytes 1048576 | tf_op jit(solution)/shard_map/all_to_all | solution.py:49
  55.1 0.1 all_to_all.55
  55.2 0.3 fusion.34
  55.5 0.3 fusion.35
  55.8 42.0 %all-reduce.1 = (f32[64,64]{1,0:T(8,128)S(1)}, f32[]{:T(128)}, f32[64,64]{1,0:T(8,128)S(1)}) all-reduce(f32[64,64]{1,0:T(8,128)S(1)} %fusion.34, f32[]{:T(128)} %get-tuple-element.8, f32[64,64]{1,0:T(8,128)S(1)} %fusion.35), channel_id=1, replica_groups=mesh['mem'=16,'rep'=2] {'mem','rep'}, use_global_device_ids=true, to_apply=%region_1.2 | all-reduce | flops 8193 | bytes 65544 | tf_op jit(solution)/shard_map/psum | solution.py:62
  98.5 0.1 copy.18
  98.6 5.8 %cholesky.16 = f32[64,64]{1,0:T(8,128)S(1)} custom-call(f32[64,64]{1,0:T(8,128)S(1)} %fusion.25), custom_call_target="Cholesky" | custom-call | tf_op jit(solution)/shard_map/jit(cholesky)/cholesky | solution.py:70
  104.5 0.6 compare_reduce_fusion
  105.2 0.7 fusion.21
  105.8 4.9 %custom-call.10 = f32[1,64,64]{1,2,0:T(8,128)S(1)} custom-call(f32[1,64,64]{2,1,0:T(8,128)S(1)} %fusion.21), custom_call_target="InvertDiagBlocksLowerTriangular" | custom-call | tf_op jit(solution)/shard_map/jit(_solve_triangular)/triangular_solve | solution.py:72
  110.7 0.2 fusion.23
  110.9 0.2 fusion.5
  111.0 39.9 %all-gather = bf16[32,2,64]{2,1,0:T(2,128)(2,1)S(1)} all-gather(bf16[1,2,64]{2,1,0:T(2,128)(2,1)S(1)} %fusion.5), channel_id=1, replica_groups=mesh['mem'=16,'rep'=2] {'mem','rep'}, dimensions={0}, use_global_device_ids=true | all-gather | bytes 8448 | tf_op jit(solution)/shard_map/all_gather | solution.py:77
  150.9 0.0 all-to-all-done
  150.9 0.1 convert_bitcast_fusion
  151.0 0.4 reshape.70
  151.4 0.2 convert_reduce_fusion
  151.6 0.3 fusion
  151.9 0.2 all_to_all.56
  152.1 18.1 %all_to_all.64 = bf16[16,4,4096]{2,1,0:T(4,128)(2,1)S(1)} all-to-all(bf16[16,4,4096]{2,1,0:T(4,128)(2,1)S(1)} %all_to_all.56), channel_id=1, replica_groups=mesh['mem'=16,'rep'=2] {'mem'}, dimensions={0} | all-to-all | bytes 1048576 | tf_op jit(solution)/shard_map/all_to_all | solution.py:82
  170.2 0.8 copy.22
  (5 shorter events, 0.1 us)
Async XLA Ops:
  0.0 3.0 %copy-start.2 = (bf16[2,1024,256]{2,1,0:T(8,128)(2,1)S(1)}, bf16[2,1024,256]{2,1,0:T(8,128)(2,1)}, u32[]{:S(2)}) copy-start(bf16[2,1024,256]{2,1,0:T(8,128)(2,1)} %param.12) | copy-start | bytes 3145732
  9.4 23.4 %all-to-all-start.1 = ((bf16[4,16,4096]{2,0,1:T(4,128)(2,1)}), bf16[4,16,4096]{2,0,1:T(4,128)(2,1)S(1)}, u32[]{:S(2)}, u32[]{:S(2)}) async-start(bf16[4,16,4096]{2,0,1:T(4,128)(2,1)} %copy.17), calls=%async_computation.1 | async-start | bytes 1048576 | tf_op jit(solution)/shard_map/all_to_all | solution.py:50
  17.8 1.0 copy-start
  17.8 1.1 copy-start.1
  20.7 16.3 %dynamic-slice-start = ((f32[65536]{0:T(1024)}, s32[]{:T(128)}), f32[4096]{0:T(1024)S(1)}, s32[]{:S(2)}) async-start(f32[65536]{0:T(1024)} %param.9, s32[]{:T(128)} %select_n.7), calls=%async_computation.4 | async-start | bytes 33280 | tf_op jit(solution)/shard_map/dynamic_slice | solution.py:54
  32.8 18.4 %all-to-all-start.2 = ((bf16[4,16,4096]{2,0,1:T(4,128)(2,1)}), bf16[4,16,4096]{2,0,1:T(4,128)(2,1)S(1)}, u32[]{:S(2)}, u32[]{:S(2)}) async-start(bf16[4,16,4096]{2,0,1:T(4,128)(2,1)} %bitcast.14), calls=%async_computation.2 | async-start | bytes 1048576 | tf_op jit(solution)/shard_map/all_to_all | solution.py:51
  51.2 99.7 %all-to-all-start = ((bf16[4,16,4096]{2,0,1:T(4,128)(2,1)}), bf16[4,16,4096]{2,0,1:T(4,128)(2,1)S(1)}, u32[]{:S(2)}, u32[]{:S(2)}) async-start(bf16[4,16,4096]{2,0,1:T(4,128)(2,1)} %bitcast), calls=%async_computation | async-start | bytes 1048576 | tf_op jit(solution)/shard_map/all_to_all | solution.py:49
where the time goes:
time: 172 us; the launch traced here: 171 us
  blocking collectives  100 us (58%)
  waiting for transfers between devices  25.5 us (15%)
  starting transfers between devices  16.2 us (9%)
  other arithmetic  15.1 us (9%)
  local copies, waits for them, and re-layouts  7.34 us (4%)
  matrix products  6.07 us (4%)
    psum x1, blocking collectives, body(): gram = lax.psum(contract(weighted, pred_dev), ('mem', 'rep')) / state_total  42 us
    all_gather x1, blocking collectives, body(): lax.all_gather(mixing, ('mem', 'rep'), axis=0, tiled=True)  39.9 us
    all_to_all x1, blocking collectives, body(): return lax.all_to_all(fresh, 'mem', split_axis=0, concat_axis=1, tiled=True)  18.1 us
    all_to_all x1, waiting for transfers between devices, body(): lax.all_to_all(resid, 'mem', split_axis=1, concat_axis=0, tiled=True)  13.4 us
    all_to_all x1, waiting for transfers between devices, body(): lax.all_to_all(particle_outcomes, 'mem', split_axis=1, concat_axis=0, til...  12.1 us
    all_to_all x1, starting transfers between devices, body(): lax.all_to_all(particle_outcomes, 'mem', split_axis=1, concat_axis=0, til...  8.34 us
    another operation x3, other arithmetic, body(): factor = jnp.linalg.cholesky(kmat)  6.52 us
    another operation x2, other arithmetic, body(): jax.scipy.linalg.solve_triangular(factor, middle, lower=True, trans='T')  5.55 us
  transfers between devices with their start and end apart: 3, of which 2 were waited for; matrix products, arithmetic and copies ran while one was open for 10% of the time, Pallas kernels for 0%

commit v1 on v0

--- a/solution.py
+++ b/solution.py
@@ -59,7 +59,7 @@
     state_wide = own_states.astype(jnp.float32)
     state_dev = (state_wide - jnp.mean(state_wide, axis=0)).astype(jnp.bfloat16)
     weighted = (pred_dev.astype(jnp.float32) * prec_block).astype(jnp.bfloat16)
-    gram = lax.psum(contract(weighted, pred_dev), ("mem", "rep")) / state_total
+    gram = lax.psum(lax.psum(contract(weighted, pred_dev), "rep"), "mem") / state_total
     cross = (
         lax.psum_scatter(
             contract(own_resid, weighted), ("mem", "rep"), scatter_dimension=0, tiled=True

time: 172 us -> 239 us (1.39)
  blocking collectives: 100 us -> 181 us
  waiting for transfers between devices: 25.5 us -> 12.1 us
    psum x1 -> x3, blocking collectives: 42 us -> 122 us  [the longest x1 77.5 us: body(): lax.psum(lax.psum(contract(weighted, pred_dev), 'rep'), 'mem') / state_total]
    all_to_all x1, waiting for transfers between devices: 13.4 us -> 0.01 us  [body(): lax.all_to_all(resid, 'mem', split_axis=1, concat_axis=0, tiled=True)]
  transfers between devices with their start and end apart: 3 -> 3, of which waited for: 2 -> 1; matrix products, arithmetic and copies ran while one was open for 10% -> 7% of each run, Pallas kernels for 0% -> 0%
where the time goes in v1:
time: 239 us; the launch traced here: 238 us
  blocking collectives  181 us (76%)
  starting transfers between devices  15.9 us (7%)
  other arithmetic  15.1 us (6%)
  waiting for transfers between devices  12.1 us (5%)
  local copies, waits for them, and re-layouts  7.34 us (3%)
  matrix products  6.07 us (3%)
    psum x1, blocking collectives, body(): lax.psum(lax.psum(contract(weighted, pred_dev), 'rep'), 'mem') / state_total  77.5 us
    psum x1, blocking collectives, body(): lax.psum(misfit_local, ('mem', 'rep')) / (member_total * state_total)  41.4 us
    all_gather x1, blocking collectives, body(): lax.all_gather(mixing, ('mem', 'rep'), axis=0, tiled=True)  40.3 us
    all_to_all x1, blocking collectives, body(): return lax.all_to_all(fresh, 'mem', split_axis=0, concat_axis=1, tiled=True)  18.1 us
    all_to_all x1, waiting for transfers between devices, body(): lax.all_to_all(particle_outcomes, 'mem', split_axis=1, concat_axis=0, til...  12.1 us
    all_to_all x1, starting transfers between devices, body(): lax.all_to_all(particle_outcomes, 'mem', split_axis=1, concat_axis=0, til...  8.34 us
    another operation x3, other arithmetic, body(): factor = jnp.linalg.cholesky(kmat)  6.52 us
    another operation x2, other arithmetic, body(): jax.scipy.linalg.solve_triangular(factor, middle, lower=True, trans='T')  5.55 us
  transfers between devices with their start and end apart: 3, of which 1 were waited for; matrix products, arithmetic and copies ran while one was open for 7% of the time, Pallas kernels for 0%

profile of v1, /device:TPU:0, one launch (start us, length us, event | category | flops | bytes accessed | tf_op | source)
XLA Modules:
  0.0 238.0 jit_solution(13207978428760311363)
XLA Ops:
  0.0 0.0 copy-start.2
  0.0 0.8 fusion.32
  0.8 0.8 fusion.33
  1.6 1.4 reshape.69
  3.0 0.0 copy-done.2
  3.0 2.5 %fusion.3 = bf16[1024,256]{1,0:T(8,128)(2,1)S(1)} fusion(bf16[1024,256]{1,0:T(8,128)(2,1)S(1)} %reshape.69, f32[1024]{0:T(1024)S(1)} %bitcast.55, f32[256]{0:T(256)S(1)} %bitcast.57, bf16[2,1024,256]{2,1,0:T(8,128)(2,1)S(1)} %copy-done.2, bf16[2,256,1024]{2,1,0:T(8,128)(2,1)} %param.10), kind=kOutput, calls=%fused_computation.12 | convolution fusion | flops 1081081856 | bytes 2626560 | tf_op jit(solution)/shard_map/dot_general | solution.py:35
  5.5 2.5 %fusion.4 = bf16[1024,256]{1,0:T(8,128)(2,1)S(1)} fusion(bf16[1024,256]{1,0:T(8,128)(2,1)S(1)} %fusion.3, f32[1024]{0:T(1024)S(1)} %bitcast.54, f32[256]{0:T(256)S(1)} %bitcast.56, bf16[2,1024,256]{2,1,0:T(8,128)(2,1)S(1)} %copy-done.2, bf16[2,256,1024]{2,1,0:T(8,128)(2,1)} %param.10), kind=kOutput, calls=%fused_computation.13 | convolution fusion | flops 1081081856 | bytes 2626560 | tf_op jit(solution)/shard_map/dot_general | solution.py:35
  8.0 0.2 all_to_all.50
  8.2 1.2 copy.17
  9.4 8.3 %all-to-all-start.1 = ((bf16[4,16,4096]{2,0,1:T(4,128)(2,1)}), bf16[4,16,4096]{2,0,1:T(4,128)(2,1)S(1)}, u32[]{:S(2)}, u32[]{:S(2)}) async-start(bf16[4,16,4096]{2,0,1:T(4,128)(2,1)} %copy.17), calls=%async_computation.1 | async-start | bytes 1048576 | tf_op jit(solution)/shard_map/all_to_all | solution.py:50
  17.8 0.0 copy-start
  17.8 0.0 copy-start.1
  17.8 0.5 reshape.71
  18.3 0.5 copy-done
  18.8 0.1 copy-done.1
  18.9 1.9 multiply_reduce_fusion
  20.7 0.0 dynamic-slice-start
  20.7 12.1 %all-to-all-done.1 = bf16[4,16,4096]{2,0,1:T(4,128)(2,1)S(1)} async-done(((bf16[4,16,4096]{2,0,1:T(4,128)(2,1)}), bf16[4,16,4096]{2,0,1:T(4,128)(2,1)S(1)}, u32[]{:S(2)}, u32[]{:S(2)}) %all-to-all-start.1) | async-done | bytes 524320 | tf_op jit(solution)/shard_map/all_to_all | solution.py:50
  32.8 3.9 %all-to-all-start.2 = ((bf16[4,16,4096]{2,0,1:T(4,128)(2,1)}), bf16[4,16,4096]{2,0,1:T(4,128)(2,1)S(1)}, u32[]{:S(2)}, u32[]{:S(2)}) async-start(bf16[4,16,4096]{2,0,1:T(4,128)(2,1)} %bitcast.14), calls=%async_computation.2 | async-start | bytes 1048576 | tf_op jit(solution)/shard_map/all_to_all | solution.py:51
  36.8 0.2 convert_reduce_fusion.1
  37.1 0.0 dynamic-slice-done
  37.1 0.5 multiply_convert_fusion.2
  37.6 0.1 convert_element_type.101
  37.7 0.1 convert_element_type.102
  37.9 0.3 fusion.34
  38.2 3.4 %psum.21 = f32[64,64]{1,0:T(8,128)S(1)} all-reduce(f32[64,64]{1,0:T(8,128)S(1)} %fusion.34), channel_id=1, replica_groups=mesh['mem'=16,'rep'=2] {'rep'}, use_global_device_ids=true, to_apply=%region_1.2 | all-reduce | flops 4096 | bytes 32768 | tf_op jit(solution)/shard_map/psum | solution.py:62
  41.6 77.5 %psum.22 = f32[64,64]{1,0:T(8,128)S(1)} all-reduce(f32[64,64]{1,0:T(8,128)S(1)} %psum.21), channel_id=1, replica_groups=mesh['mem'=16,'rep'=2] {'mem'}, use_global_device_ids=true, to_apply=%region_2.3 | all-reduce | flops 4096 | bytes 32768 | tf_op jit(solution)/shard_map/psum | solution.py:62
  119.0 0.0 all-to-all-done.2
  119.0 3.6 %all-to-all-start = ((bf16[4,16,4096]{2,0,1:T(4,128)(2,1)}), bf16[4,16,4096]{2,0,1:T(4,128)(2,1)S(1)}, u32[]{:S(2)}, u32[]{:S(2)}) async-start(bf16[4,16,4096]{2,0,1:T(4,128)(2,1)} %bitcast), calls=%async_computation | async-start | bytes 1048576 | tf_op jit(solution)/shard_map/all_to_all | solution.py:49
  122.6 0.1 all_to_all.55
  122.8 0.3 fusion.35
  123.0 41.4 %all-reduce.1 = (f32[]{:T(128)}, f32[64,64]{1,0:T(8,128)S(1)}) all-reduce(f32[]{:T(128)} %get-tuple-element.7, f32[64,64]{1,0:T(8,128)S(1)} %fusion.35), channel_id=1, replica_groups=mesh['mem'=16,'rep'=2] {'mem','rep'}, use_global_device_ids=true, to_apply=%region_4.5 | all-reduce | flops 4097 | bytes 32776 | tf_op jit(solution)/shard_map/psum | solution.py:47
  165.1 0.1 copy.18
  165.2 5.8 %cholesky.16 = f32[64,64]{1,0:T(8,128)S(1)} custom-call(f32[64,64]{1,0:T(8,128)S(1)} %fusion.25), custom_call_target="Cholesky" | custom-call | tf_op jit(solution)/shard_map/jit(cholesky)/cholesky | solution.py:70
  171.1 0.6 compare_reduce_fusion
  171.7 0.7 fusion.21
  172.4 4.9 %custom-call.10 = f32[1,64,64]{1,2,0:T(8,128)S(1)} custom-call(f32[1,64,64]{2,1,0:T(8,128)S(1)} %fusion.21), custom_call_target="InvertDiagBlocksLowerTriangular" | custom-call | tf_op jit(solution)/shard_map/jit(_solve_triangular)/triangular_solve | solution.py:72
  177.3 0.2 fusion.23
  177.4 0.2 fusion.5
  177.6 40.3 %all-gather = bf16[32,2,64]{2,1,0:T(2,128)(2,1)S(1)} all-gather(bf16[1,2,64]{2,1,0:T(2,128)(2,1)S(1)} %fusion.5), channel_id=1, replica_groups=mesh['mem'=16,'rep'=2] {'mem','rep'}, dimensions={0}, use_global_device_ids=true | all-gather | bytes 8448 | tf_op jit(solution)/shard_map/all_gather | solution.py:77
  217.9 0.0 all-to-all-done
  217.9 0.1 convert_bitcast_fusion
  218.0 0.4 reshape.70
  218.4 0.2 convert_reduce_fusion
  218.6 0.3 fusion
  218.9 0.2 all_to_all.56
  219.1 18.1 %all_to_all.64 = bf16[16,4,4096]{2,1,0:T(4,128)(2,1)S(1)} all-to-all(bf16[16,4,4096]{2,1,0:T(4,128)(2,1)S(1)} %all_to_all.56), channel_id=1, replica_groups=mesh['mem'=16,'rep'=2] {'mem'}, dimensions={0} | all-to-all | bytes 1048576 | tf_op jit(solution)/shard_map/all_to_all | solution.py:82
  237.2 0.8 copy.22
  (5 shorter events, 0.1 us)
Async XLA Ops:
  0.0 3.0 %copy-start.2 = (bf16[2,1024,256]{2,1,0:T(8,128)(2,1)S(1)}, bf16[2,1024,256]{2,1,0:T(8,128)(2,1)}, u32[]{:S(2)}) copy-start(bf16[2,1024,256]{2,1,0:T(8,128)(2,1)} %param.12) | copy-start | bytes 3145732
  9.4 23.4 %all-to-all-start.1 = ((bf16[4,16,4096]{2,0,1:T(4,128)(2,1)}), bf16[4,16,4096]{2,0,1:T(4,128)(2,1)S(1)}, u32[]{:S(2)}, u32[]{:S(2)}) async-start(bf16[4,16,4096]{2,0,1:T(4,128)(2,1)} %copy.17), calls=%async_computation.1 | async-start | bytes 1048576 | tf_op jit(solution)/shard_map/all_to_all | solution.py:50
  17.8 1.0 copy-start
  17.8 1.1 copy-start.1
  20.7 16.3 %dynamic-slice-start = ((f32[65536]{0:T(1024)}, s32[]{:T(128)}), f32[4096]{0:T(1024)S(1)}, s32[]{:S(2)}) async-start(f32[65536]{0:T(1024)} %param.9, s32[]{:T(128)} %select_n.7), calls=%async_computation.4 | async-start | bytes 33280 | tf_op jit(solution)/shard_map/dynamic_slice | solution.py:54
  32.8 86.2 %all-to-all-start.2 = ((bf16[4,16,4096]{2,0,1:T(4,128)(2,1)}), bf16[4,16,4096]{2,0,1:T(4,128)(2,1)S(1)}, u32[]{:S(2)}, u32[]{:S(2)}) async-start(bf16[4,16,4096]{2,0,1:T(4,128)(2,1)} %bitcast.14), calls=%async_computation.2 | async-start | bytes 1048576 | tf_op jit(solution)/shard_map/all_to_all | solution.py:51
  119.0 98.8 %all-to-all-start = ((bf16[4,16,4096]{2,0,1:T(4,128)(2,1)}), bf16[4,16,4096]{2,0,1:T(4,128)(2,1)S(1)}, u32[]{:S(2)}, u32[]{:S(2)}) async-start(bf16[4,16,4096]{2,0,1:T(4,128)(2,1)} %bitcast), calls=%async_computation | async-start | bytes 1048576 | tf_op jit(solution)/shard_map/all_to_all | solution.py:49
